TPU v7x, 32 devices: a whole 2x2x4 slice. The times are simulated.
32 devices in a mesh: segment: 4 (over y, core), dp: 8 (over z, x).
Axes of the slice: x: 2, y: 2, z: 4, core: 2. Of those that a mesh axis runs over, the one named last changes fastest.
Arguments:
- token_ids: int32 [1024], P('dp'), may hold values from 0 to 38015, as said below
- table: bfloat16 [4752, 28672], P('segment', 'dp'), may hold values from -6 to 6
- out_grad: bfloat16 [1024, 3584], P('dp', 'segment'), may hold values from -6 to 6
Outputs:
- embedded: bfloat16 [1024, 3584], P('dp')
- table_grad: bfloat16 [4752, 28672], P('segment', 'dp')
Inputs may be any that keep to these rules, and one draw needn't show every extreme that they name: `token_ids`: in the 128 tokens of each data group, at most 16 ids lie in one segment's slice of 9504 rows with one residue modulo 8; in every data group some segment and residue has exactly 16.
All inputs are finite; a program needn't handle non-finite values.
Results may differ from a plain program's by a relative error of at most 0.001.
Values may be sent and summed in bfloat16 or wider, within the bound.
A program may use at most 64 MiB of HBM per device.

v0:
```python
import jax
import jax.numpy as jnp
from jax import lax
from jax.sharding import PartitionSpec as P

D = 3584
PACK = 8


def body(token_ids, table, out_grad):
    lines = table.shape[0]
    width = table.shape[1]
    groups = lax.axis_size("dp")
    tok_rows = token_ids.shape[0]
    quarters = D // width
    slot = lax.axis_index("dp") // quarters
    first = lax.axis_index("segment") * lines * PACK
    every_id = lax.all_gather(token_ids, "dp", axis=0, tiled=True)
    local = every_id - first
    in_section = (local >= 0) & (local < lines * PACK)
    owned = in_section & (local % PACK == slot)
    line_idx = jnp.clip(local // PACK, 0, lines - 1)
    whole_grad = lax.all_gather(out_grad, "segment", axis=1, tiled=True)
    capacity = tok_rows // PACK
    owned_grid = owned.reshape(groups, tok_rows)
    rank = jnp.cumsum(owned_grid.astype(jnp.int32), axis=1) - 1
    place = jnp.where(owned_grid, rank, capacity)
    group_rows = jnp.broadcast_to(jnp.arange(groups, dtype=jnp.int32)[:, None], (groups, tok_rows))
    row_of = (
        jnp.zeros((groups, capacity), jnp.int32)
        .at[group_rows, place]
        .set(line_idx.reshape(groups, tok_rows), mode="drop")
    )
    filled = jnp.zeros((groups, capacity), jnp.bool_).at[group_rows, place].set(True, mode="drop")
    fetched = jnp.take(table, row_of.reshape(-1), axis=0).reshape(groups, capacity, width)
    fetched = jnp.where(filled[:, :, None], fetched, jnp.zeros((), jnp.bfloat16))
    arrived = lax.all_to_all(fetched, "dp", split_axis=0, concat_axis=0, tiled=True)
    my_local = token_ids - first
    my_in = (my_local >= 0) & (my_local < lines * PACK)
    my_slot = my_local % PACK
    slot_hits = (my_slot[:, None] == jnp.arange(PACK, dtype=jnp.int32)[None, :]) & my_in[:, None]
    slot_ranks = jnp.cumsum(slot_hits.astype(jnp.int32), axis=0) - 1
    my_rank = jnp.sum(jnp.where(slot_hits, slot_ranks, 0), axis=1)
    sources = my_slot[:, None] * quarters + jnp.arange(quarters, dtype=jnp.int32)[None, :]
    flat_index = jnp.clip(sources * capacity + my_rank[:, None], 0, groups * capacity - 1)
    gathered = jnp.take(
        arrived.reshape(groups * capacity, width), flat_index.reshape(-1), axis=0
    ).reshape(tok_rows, D)
    segment_part = jnp.where(my_in[:, None], gathered.astype(jnp.float32), 0.0)
    slot_place = jnp.where(my_in, my_slot, PACK)
    token_at = (
        jnp.zeros((PACK, capacity), jnp.int32)
        .at[slot_place, my_rank]
        .set(jnp.arange(tok_rows, dtype=jnp.int32), mode="drop")
    )
    valid = jnp.zeros((PACK, capacity), jnp.bool_).at[slot_place, my_rank].set(True, mode="drop")
    grad_pick = jnp.take(whole_grad, token_at.reshape(-1), axis=0).reshape(
        PACK, capacity, quarters, width
    )
    grad_pick = jnp.where(valid[:, :, None, None], grad_pick, jnp.zeros((), jnp.bfloat16))
    grad_send = grad_pick.transpose(0, 2, 1, 3).reshape(groups, capacity, width)
    returned = lax.all_to_all(grad_send, "dp", split_axis=0, concat_axis=0, tiled=True)
    target = jnp.where(filled, row_of, lines)
    accum = (
        jnp.zeros((lines, width), jnp.float32)
        .at[target.reshape(-1)]
        .add(returned.reshape(-1, width).astype(jnp.float32), mode="drop")
    )
    embedded = lax.psum(segment_part.astype(jnp.bfloat16), "segment")
    return (embedded, accum.astype(jnp.bfloat16))


def solution(mesh):
    placed = (P("dp"), P("segment", "dp"), P("dp", "segment"))
    return jax.shard_map(
        body,
        mesh=mesh,
        in_specs=placed,
        out_specs=(P("dp", None), P("segment", "dp")),
        check_vma=False,
    )
```

profile of v0, /device:TPU:0, one launch (start us, length us, event | category | flops | bytes accessed | tf_op | source)
XLA Modules:
  0.0 159.1 jit_solution(7434590179938538914)
XLA Ops:
  7.2 22.6 %all-gather = s32[8,1,128]{2,1,0:T(1,128)S(1)} all-gather(s32[1,1,128]{2,1,0:T(1,128)} %bitcast.39), channel_id=1, replica_groups=mesh['segment'=4,'dp'=8] {'dp'}, dimensions={0}, use_global_device_ids=true | all-gather | bytes 4608 | tf_op jit(solution)/shard_map/all_gather | solution.py:18
  29.8 0.3 copy.12
  30.1 0.3 copy.13
  30.4 23.6 %compare_select_fusion = s32[8,128,1]{2,0,1:T(8,128)S(1)} fusion(pred[8,128,1]{2,0,1:T(8,128)(4,1)S(1)} %copy.13, s32[8,128,1]{2,0,1:T(8,128)S(1)} %copy.12), kind=kOutput, calls=%fused_computation.12 | output fusion | flops 135168 | bytes 9216 | tf_op jit(solution)/shard_map/jit(cumsum)/reduce_window_sum | solution.py:26
  54.0 0.2 copy.14
  54.2 0.8 multiply_reduce_fusion
  55.0 0.1 copy.19
  55.1 0.7 and_reduce_fusion
  55.8 0.1 copy.18
  56.0 4.3 %scatter_custom_fusion.4 = s32[128]{0:T(128)S(1)} fusion(s32[1024]{0:T(1024)S(1)} %bitcast.40, s32[1024]{0:T(1024)S(1)} %fusion.6, s32[]{:T(128)} %constant.70.clone.1), kind=kCustom, calls=%fused_computation.66 | custom fusion | bytes 516
  60.4 4.3 %scatter_custom_fusion.3 = pred[128]{0:T(512)(128)(4,1)S(1)} fusion(s32[1024]{0:T(1024)S(1)} %bitcast.41, pred[1024]{0:T(1024)(128)(4,1)S(1)} %broadcast.224, pred[]{:T(512)} %constant.71.clone.1), kind=kCustom, calls=%fused_computation.56 | custom fusion | bytes 129
  64.8 0.1 reshape.185
  64.9 6.6 %gather_fusion = bf16[128,3584]{1,0:T(8,128)(2,1)S(1)} fusion(bf16[1188,3584]{1,0:T(8,128)(2,1)} %param.6, s32[1024]{0:T(1024)S(1)} %pad_clamp_fusion.2), kind=kCustom, calls=%fused_computation.2 | custom fusion | bytes 1835520 | tf_op jit(solution)/shard_map/jit(_take)/gather | solution.py:35
  71.4 1.1 select_select_fusion
  72.6 3.6 %all-to-all-start = ((bf16[8,16,3584]{2,1,0:T(8,128)(2,1)}), bf16[8,16,3584]{2,1,0:T(8,128)(2,1)S(1)}, u32[]{:S(2)}, u32[]{:S(2)}) async-start(bf16[8,16,3584]{2,1,0:T(8,128)(2,1)} %select_select_fusion), calls=%async_computation | async-start | bytes 1835008 | tf_op jit(solution)/shard_map/all_to_all | solution.py:37
  76.2 0.1 fusion.4
  76.3 0.2 reduce_window_sum.23
  76.4 0.2 select_reduce_fusion
  76.7 6.4 %scatter_fusion.1 = s32[8,16]{1,0:T(8,128)S(1)} fusion(s32[8,16]{1,0:T(8,128)S(1)} %broadcast.169, s32[128]{0:T(128)S(1)} %fusion.18, s32[128]{0:T(128)S(1)} %iota.14), kind=kCustom, calls=%fused_computation.4 | custom fusion | bytes 2560 | tf_op jit(solution)/shard_map/scatter | solution.py:54
  83.0 0.1 reshape.180
  83.2 9.5 %all_gather.7 = bf16[128,3584]{1,0:T(8,128)(2,1)S(1)} all-gather(bf16[128,896]{1,0:T(8,128)(2,1)S(1)} %copy-done), channel_id=1, replica_groups=mesh['segment'=4,'dp'=8] {'segment'}, dimensions={1}, use_global_device_ids=true | all-gather | bytes 1146880 | tf_op jit(solution)/shard_map/all_gather | solution.py:23
  92.7 1.1 gather_fusion.2
  93.8 6.5 %scatter_fusion = pred[8,16]{1,0:T(8,128)(4,1)S(1)} fusion(pred[8,16]{1,0:T(8,128)(4,1)S(1)} %broadcast.166, s32[128]{0:T(128)S(1)} %fusion.18, pred[128]{0:T(512)(128)(4,1)S(1)} %broadcast.225), kind=kCustom, calls=%fused_computation.3 | custom fusion | bytes 1408 | tf_op jit(solution)/shard_map/scatter | solution.py:56
  100.3 0.2 broadcast_select_fusion
  100.5 1.1 broadcast_select_fusion.1
  101.5 5.9 %all-to-all-start.1 = ((bf16[8,16,3584]{2,1,0:T(8,128)(2,1)}), bf16[8,16,3584]{2,1,0:T(8,128)(2,1)S(1)}, u32[]{:S(2)}, u32[]{:S(2)}) async-start(bf16[8,16,3584]{2,1,0:T(8,128)(2,1)} %broadcast_select_fusion.1), calls=%async_computation.1 | async-start | bytes 1835008 | tf_op jit(solution)/shard_map/all_to_all | solution.py:62
  107.5 1.1 gather_fusion.1
  108.7 1.3 select_convert_fusion
  110.0 20.9 %all-to-all-done.1 = bf16[8,16,3584]{2,1,0:T(8,128)(2,1)S(1)} async-done(((bf16[8,16,3584]{2,1,0:T(8,128)(2,1)}), bf16[8,16,3584]{2,1,0:T(8,128)(2,1)S(1)}, u32[]{:S(2)}, u32[]{:S(2)}) %all-to-all-start.1) | async-done | bytes 917536 | tf_op jit(solution)/shard_map/all_to_all | solution.py:62
  130.9 10.0 %scatter_custom_fusion.2 = f32[1188,3584]{1,0:T(8,128)} fusion(s32[128]{0:T(128)S(1)} %fusion.16, f32[]{:T(128)} %constant.121.clone.1, bf16[128,3584]{1,0:T(8,128)(2,1)S(1)} %bitcast.35), kind=kCustom, calls=%fused_computation.8 | custom fusion | flops 917504 | bytes 17948676 | tf_op jit(solution)/shard_map/scatter-add | solution.py:67
  140.9 9.1 %convert_element_type.32 = bf16[1188,3584]{1,0:T(8,128)(2,1)} convert(f32[1188,3584]{1,0:T(8,128)} %scatter_custom_fusion.2) | non-fusion elementwise | flops 4257792 | bytes 25546752 | tf_op jit(solution)/shard_map/convert_element_type | solution.py:70
  150.1 2.2 %copy.23 = bf16[128,3584]{1,0:T(8,128)(2,1)} copy(bf16[128,3584]{1,0:T(8,128)(2,1)} %all-reduce.2.cloned.1.call-done) | data formatting | bytes 1835008
  (34 shorter events, 0.5 us)
Async XLA Ops:
  7.2 69.0 %copy-start.1 = (s32[128]{0:T(128)S(1)}, s32[128]{0:T(128)}, u32[]{:S(2)}) copy-start(s32[128]{0:T(128)} %param.5) | copy-start | bytes 1540
  7.2 76.0 %copy-start = (bf16[128,896]{1,0:T(8,128)(2,1)S(1)}, bf16[128,896]{1,0:T(8,128)(2,1)}, u32[]{:S(2)}) copy-start(bf16[128,896]{1,0:T(8,128)(2,1)} %param.7) | copy-start | bytes 688132
  72.6 29.0 %all-to-all-start = ((bf16[8,16,3584]{2,1,0:T(8,128)(2,1)}), bf16[8,16,3584]{2,1,0:T(8,128)(2,1)S(1)}, u32[]{:S(2)}, u32[]{:S(2)}) async-start(bf16[8,16,3584]{2,1,0:T(8,128)(2,1)} %select_select_fusion), calls=%async_computation | async-start | bytes 1835008 | tf_op jit(solution)/shard_map/all_to_all | solution.py:37
  101.5 29.4 %all-to-all-start.1 = ((bf16[8,16,3584]{2,1,0:T(8,128)(2,1)}), bf16[8,16,3584]{2,1,0:T(8,128)(2,1)S(1)}, u32[]{:S(2)}, u32[]{:S(2)}) async-start(bf16[8,16,3584]{2,1,0:T(8,128)(2,1)} %broadcast_select_fusion.1), calls=%async_computation.1 | async-start | bytes 1835008 | tf_op jit(solution)/shard_map/all_to_all | solution.py:62
  107.5 42.6 %all-reduce.2.cloned.1.call-start = ((), (), s32[]{:S(2)}) async-start(), calls=%async_computation.2 | async-start | bytes 1835008 | tf_op jit(solution)/shard_map/psum | solution.py:69
Sparse Core Ops, SparseCore 0:
  111.2 36.1 all-reduce.1
where the time goes:
time: 159 us
  other arithmetic  48.5 us (31%)
  local copies, waits for them, and re-layouts  33.8 us (21%)
  blocking collectives  32.1 us (20%)
  waiting for transfers between devices  20.9 us (13%)
  between operations  14.3 us (9%)
  starting transfers between devices  9.51 us (6%)
    another operation x1, other arithmetic, body(): rank = jnp.cumsum(owned_grid.astype(jnp.int32), axis=1) - 1  23.6 us
    all_gather x1, blocking collectives, body(): every_id = lax.all_gather(token_ids, 'dp', axis=0, tiled=True)  22.6 us
    all_to_all x1, waiting for transfers between devices, body(): lax.all_to_all(grad_send, 'dp', split_axis=0, concat_axis=0, tiled=True)  20.9 us
    unnamed x11, local copies, waits for them, and re-layouts  11.1 us
    scatter-add x1, other arithmetic, body(): accum = jnp.zeros((lines, width), jnp.float32).at[target.reshape(-1)].add...  10 us
    all_gather x1, blocking collectives, body(): whole_grad = lax.all_gather(out_grad, 'segment', axis=1, tiled=True)  9.52 us
    convert_element_type x1, other arithmetic, body(): return (embedded, accum.astype(jnp.bfloat16))  9.14 us
    gather x1, local copies, waits for them, and re-layouts, body(): jnp.take(table, row_of.reshape(-1), axis=0).reshape(groups, capacity, width)  6.55 us
  transfers between devices with their start and end apart: 3, of which 1 were waited for; matrix products, arithmetic and copies ran while one was open for 24% of the time, Pallas kernels for 0%

commit v1 on v0

v1 whole, which is shorter than its diff:
```python
import functools

import jax
import jax.numpy as jnp
from jax import lax
from jax.experimental import pallas as pl
from jax.experimental.pallas import tpu as pltpu
from jax.sharding import PartitionSpec as P

PACK = 8
BF = jnp.bfloat16
F32 = jnp.float32


def flip(index, bit):
    return index + bit - 2 * bit * ((index // bit) % 2)


def push(src, dst, send, recv, peer):
    copy = pltpu.make_async_remote_copy(
        src_ref=src,
        dst_ref=dst,
        send_sem=send,
        recv_sem=recv,
        device_id=peer,
        device_id_type=pl.DeviceIdType.MESH,
    )
    copy.start()
    return copy


def select(ids, first, lines, slot, cap):
    rows, tok = ids.shape
    local = ids - first
    owned = (local >= 0) & (local < lines * PACK) & (ids % PACK == slot)
    before = lax.broadcasted_iota(jnp.int32, (tok, tok), 0) < lax.broadcasted_iota(
        jnp.int32, (tok, tok), 1
    )
    rank = jnp.dot(
        jnp.where(owned, 1.0, 0.0).astype(BF),
        jnp.where(before, 1.0, 0.0).astype(BF),
        preferred_element_type=F32,
    )
    want = lax.broadcasted_iota(jnp.int32, (rows, tok), 0) % cap
    return owned & (rank.astype(jnp.int32) == want), local


def kernel(
    groups, segs, inside, chunk,
    ids_ref, table_ref, grad_ref,
    emb_ref, back_ref, hot_ref,
    ids_all, table, rows_out, rows_in, grads, back_out, part, halves, total,
    table_sem, ids_sem, grad_sem, fwd_sem, bwd_sem, seg_sem, copy_sem,
):
    dp = lax.axis_index("dp")
    seg = lax.axis_index("segment")
    lines, width = table.shape
    cap, tok = ids_ref.shape
    quarters = groups // PACK
    chunks = width // chunk
    half = tok // 2
    first = seg * lines * PACK
    core = seg % 2
    offsets = sorted(range(1, groups), key=lambda k: -min(k, groups - k))
    bits = [1 << b for b in range(segs.bit_length() - 1)]

    load = pltpu.make_async_copy(table_ref, table, table_sem)
    load.start()
    barrier = pltpu.get_barrier_semaphore()
    for k in offsets:
        pl.semaphore_signal(
            barrier, inc=1, device_id={"dp": (dp + k) % groups},
            device_id_type=pl.DeviceIdType.MESH,
        )
    for b in bits:
        pl.semaphore_signal(
            barrier, inc=1, device_id={"segment": flip(seg, b)},
            device_id_type=pl.DeviceIdType.MESH,
        )
    pl.semaphore_wait(barrier, len(offsets) + len(bits))

    sent = []
    ids_copies = []
    for k in offsets:
        ids_copies.append(push(
            ids_ref, ids_all.at[dp], ids_sem.at[0, k], ids_sem.at[1, k],
            {"dp": (dp + k) % groups},
        ))
    ids_all[dp] = ids_ref[...]

    grad_waits = []
    if inside:
        grads[seg] = grad_ref[...]
        held = [seg]
        stage = 0
        pending = []
        far = bits[::-1]
        copies = [push(
            grad_ref, grads.at[seg], grad_sem.at[0, 0], grad_sem.at[1, 0],
            {"segment": flip(seg, far[0])},
        )]
        stage = 1
        grad_waits = copies

    mine = jnp.concatenate([ids_ref[...]] * PACK, axis=0)
    slot_of = lax.broadcasted_iota(jnp.int32, (PACK * cap, tok), 0) // cap
    pick, _ = select(mine, first, lines, slot_of, cap)
    pick = jnp.where(pick, 1.0, 0.0)
    spread = pick.T.astype(BF)
    pick = pick.astype(BF)

    for copy in ids_copies:
        copy.wait_recv()
    named, local = select(
        ids_all[...].reshape(groups * cap, tok), first, lines, dp // quarters, cap
    )
    line = jnp.sum(
        jnp.where(named, (local // PACK + 1).astype(F32), 0.0), axis=1, keepdims=True
    ).astype(jnp.int32) - 1
    hot = jnp.where(
        lax.broadcasted_iota(jnp.int32, (groups * cap, lines), 1) == line, 1.0, 0.0
    ).astype(BF)
    hot_ref[...] = hot

    load.wait()
    fwd = []
    for f in range(chunks):
        cols = pl.ds(f * chunk, chunk)
        got = jnp.dot(hot_ref[...], table[:, cols], preferred_element_type=F32).astype(BF)
        rows_out[:, :, cols] = got.reshape(groups, cap, chunk)
        for k in offsets:
            peer = (dp + k) % groups
            fwd.append(push(
                rows_out.at[peer, :, cols], rows_in.at[dp, :, cols],
                fwd_sem.at[0, k, f], fwd_sem.at[1, k, f], {"dp": peer},
            ))
    rows_in[dp] = rows_out[dp]

    if inside:
        held = [seg]
        slot = 0
        for level, b in enumerate(far):
            if level > 0:
                copies = []
                for piece in held:
                    slot += 1
                    copies.append(push(
                        grads.at[piece], grads.at[piece],
                        grad_sem.at[0, slot], grad_sem.at[1, slot], {"segment": flip(seg, b)},
                    ))
            for copy in copies:
                copy.wait_recv()
            sent += copies
            held = held + [flip(piece, b) for piece in held]
        piece_width = grads.shape[2]
    else:
        piece_width = width

    whole = quarters * width
    for f in range(whole // piece_width):
        q, off = (f * piece_width) // width, (f * piece_width) % width
        if inside:
            block = grads[f]
        else:
            block = grad_ref[:, f * piece_width:(f + 1) * piece_width]
        got = jnp.dot(pick, block, preferred_element_type=F32).astype(BF)
        for r in range(PACK):
            back_out[r * quarters + q, :, off:off + piece_width] = got[r * cap:(r + 1) * cap]
    bwd = []
    for k in offsets:
        peer = (dp + k) % groups
        bwd.append(push(
            back_out.at[peer], back_ref.at[dp], bwd_sem.at[0, k], bwd_sem.at[1, k], {"dp": peer},
        ))
    back_ref[dp] = back_out[dp]

    for copy in fwd:
        copy.wait_recv()
    for q in range(quarters):
        for f in range(chunks):
            got = jnp.concatenate(
                [rows_in[r * quarters + q, :, f * chunk:(f + 1) * chunk] for r in range(PACK)], axis=0
            )
            got = jnp.dot(spread, got, preferred_element_type=F32).astype(BF)
            at = q * width + f * chunk
            part[:, :, at:at + chunk] = got.reshape(2, half, chunk)

    copy = push(
        part.at[1 - core], halves.at[0], seg_sem.at[0, 0], seg_sem.at[1, 0],
        {"segment": flip(seg, 1)},
    )
    copy.wait_recv()
    sent.append(copy)
    total[0] = part[core] + halves[0]
    for n, b in enumerate(bits[1:]):
        copy = push(
            total.at[n], halves.at[n + 1], seg_sem.at[0, n + 1], seg_sem.at[1, n + 1],
            {"segment": flip(seg, b)},
        )
        copy.wait_recv()
        sent.append(copy)
        total[n + 1] = total[n] + halves[n + 1]
    last = len(bits) - 1
    copy = push(
        total.at[last], emb_ref.at[core], seg_sem.at[0, last + 1], seg_sem.at[1, last + 1],
        {"segment": flip(seg, 1)},
    )
    emb_ref[core] = total[last]
    copy.wait_recv()
    sent.append(copy)

    for copy in bwd:
        copy.wait_recv()
    for copy in sent + ids_copies + fwd + bwd:
        copy.wait_send()


def body(token_ids, table, out_grad, groups, segs):
    lines, width = table.shape
    tok, piece = out_grad.shape
    depth = segs * piece
    cap = tok // PACK
    inside = piece % 128 == 0 and width % piece == 0
    if not inside:
        out_grad = lax.all_gather(out_grad, "segment", axis=1, tiled=True)
    chunk = width // 4 if width % 512 == 0 else width
    chunks = width // chunk
    levels = segs.bit_length() - 1
    vmem = pl.BlockSpec(memory_space=pltpu.VMEM)
    dma = pltpu.SemaphoreType.DMA
    emb, back, hot = pl.pallas_call(
        functools.partial(kernel, groups, segs, inside, chunk),
        out_shape=(
            jax.ShapeDtypeStruct((2, tok // 2, depth), BF),
            jax.ShapeDtypeStruct((groups, cap, width), BF),
            jax.ShapeDtypeStruct((groups * cap, lines), BF),
        ),
        in_specs=[vmem, pl.BlockSpec(memory_space=pl.ANY), vmem],
        out_specs=(vmem, vmem, vmem),
        scratch_shapes=[
            pltpu.VMEM((groups, cap, tok), jnp.int32),
            pltpu.VMEM((lines, width), BF),
            pltpu.VMEM((groups, cap, width), BF),
            pltpu.VMEM((groups, cap, width), BF),
            pltpu.VMEM((segs, tok, piece) if inside else (1, 16, 128), BF),
            pltpu.VMEM((groups, cap, width), BF),
            pltpu.VMEM((2, tok // 2, depth), BF),
            pltpu.VMEM((levels, tok // 2, depth), BF),
            pltpu.VMEM((levels, tok // 2, depth), BF),
            dma,
            dma((2, groups)),
            dma((2, segs)),
            dma((2, groups, chunks)),
            dma((2, groups)),
            dma((2, levels + 1)),
            dma,
        ],
        compiler_params=pltpu.CompilerParams(
            collective_id=0, has_side_effects=True, vmem_limit_bytes=48 << 20
        ),
    )(jnp.broadcast_to(token_ids[None, :], (cap, tok)), table, out_grad)
    grad = lax.dot_general(
        hot, back.reshape(groups * cap, width), (((0,), (0,)), ((), ())),
        preferred_element_type=F32,
    )
    return emb.reshape(tok, depth), grad.astype(BF)


def solution(mesh):
    placed = (P("dp"), P("segment", "dp"), P("dp", "segment"))
    return jax.shard_map(
        functools.partial(body, groups=mesh.shape["dp"], segs=mesh.shape["segment"]),
        mesh=mesh,
        in_specs=placed,
        out_specs=(P("dp", None), P("segment", "dp")),
        check_vma=False,
    )
```

time: 159 us -> 65 us (0.41)
  Pallas kernels: 0 us -> 55.8 us
  other arithmetic: 48.5 us -> 0 us
  blocking collectives: 32.1 us -> 0 us
  local copies, waits for them, and re-layouts: 33.8 us -> 2.52 us
  waiting for transfers between devices: 20.9 us -> 0 us
  between operations: 14.3 us -> 0.64 us
  starting transfers between devices: 9.51 us -> 0 us
  matrix products: 0 us -> 5.85 us
    pallas_call x0 -> x1, Pallas kernels: none -> 55.8 us  [body(): pl.pallas_call(functools.partial(kernel, groups, segs, inside, chunk), ou...]
    all_gather x2 -> x0, blocking collectives: 32.1 us -> none  [the longest x1 22.6 us: body(): every_id = lax.all_gather(token_ids, 'dp', axis=0, tiled=True)]
    another operation x2 -> x0, other arithmetic: 23.8 us -> none  [the longest x1 23.6 us: body(): rank = jnp.cumsum(owned_grid.astype(jnp.int32), axis=1) - 1]
    all_to_all x2 -> x0, waiting for transfers between devices: 20.9 us -> none  [the longest x1 20.9 us: body(): lax.all_to_all(grad_send, 'dp', split_axis=0, concat_axis=0, tiled=True)]
    scatter x4 -> x0, local copies, waits for them, and re-layouts: 13 us -> none  [the longest x1 6.48 us: body(): jnp.zeros((PACK, capacity), jnp.bool_).at[slot_place, my_rank]]
    convert_element_type x4 -> x0, other arithmetic: 10.5 us -> none  [the longest x1 9.14 us: body(): return (embedded, accum.astype(jnp.bfloat16))]
    scatter-add x1 -> x0, other arithmetic: 10 us -> none  [body(): accum = jnp.zeros((lines, width), jnp.float32).at[target.reshape(-1)].add...]
    all_to_all x2 -> x0, starting transfers between devices: 9.47 us -> none  [the longest x1 5.92 us: body(): lax.all_to_all(grad_send, 'dp', split_axis=0, concat_axis=0, tiled=True)]
  transfers between devices with their start and end apart: 3 -> 0, of which waited for: 1 -> 0; matrix products, arithmetic and copies ran while one was open for 24% -> 0% of each run, Pallas kernels for 0% -> 0%
where the time goes in v1:
time: 65 us; the launch traced here: 64.9 us
  Pallas kernels  55.8 us (86%)
  matrix products  5.85 us (9%)
  local copies, waits for them, and re-layouts  2.52 us (4%)
    pallas_call x1, Pallas kernels, body(): pl.pallas_call(functools.partial(kernel, groups, segs, inside, chunk), ou...  55.8 us
    dot_general x1, matrix products, body(): lax.dot_general(hot, back.reshape(groups * cap, width), (((0,), (0,)), ((...  5.85 us
    unnamed x3, local copies, waits for them, and re-layouts  1.86 us

profile of v1, /device:TPU:0, one launch (start us, length us, event | category | flops | bytes accessed | tf_op | source)
XLA Modules:
  0.0 64.9 jit_solution(10038933221927238983)
XLA Ops:
  0.6 0.7 %broadcast_in_dim.2.ids_ref = s32[16,128]{1,0:T(8,128)S(1)} broadcast(s32[128]{0:T(128)} %param.3), dimensions={1} | broadcast | bytes 8704 | tf_op jit(solution)/shard_map/broadcast_in_dim | solution.py:261
  1.3 0.0 copy-start
  1.3 0.9 %copy-done = bf16[128,896]{1,0:T(8,128)(2,1)S(1)} copy-done((bf16[128,896]{1,0:T(8,128)(2,1)S(1)}, bf16[128,896]{1,0:T(8,128)(2,1)}, u32[]{:S(2)}) %copy-start) | copy-done | bytes 229400
  2.2 55.8 %shard_map.50 = (bf16[2,64,3584]{2,1,0:T(8,128)(2,1)S(1)}, bf16[8,16,3584]{2,1,0:T(8,128)(2,1)S(1)}, bf16[128,1188]{1,0:T(8,128)(2,1)S(1)}) custom-call(s32[16,128]{1,0:T(8,128)S(1)} %broadcast_in_dim.2.ids_ref, bf16[1188,3584]{1,0:T(8,128)(2,1)} %table_ref.1, bf16[128,896]{1,0:T(8,128)(2,1)S(1)} %copy-done), custom_call_target="tpu_custom_call" | custom-call | tf_op jit(solution)/shard_map/pallas_call | solution.py:231
  58.1 5.9 %convolution_convert_fusion = bf16[1188,3584]{1,0:T(8,128)(2,1)} fusion(bf16[128,1188]{1,0:T(8,128)(2,1)S(1)} %get-tuple-element.6, bf16[128,3584]{1,0:T(8,128)(2,1)S(1)} %bitcast.4), kind=kOutput, calls=%fused_computation | convolution fusion | flops 1094252544 | bytes 9737216 | tf_op jit(solution)/shard_map/dot_general | solution.py:262
  63.9 0.9 %copy.6 = bf16[128,3584]{1,0:T(8,128)(2,1)} copy(bf16[128,3584]{1,0:T(8,128)(2,1)S(1)} %bitcast.5) | data formatting | bytes 1835008
Async XLA Ops:
  1.3 0.9 %copy-start = (bf16[128,896]{1,0:T(8,128)(2,1)S(1)}, bf16[128,896]{1,0:T(8,128)(2,1)}, u32[]{:S(2)}) copy-start(bf16[128,896]{1,0:T(8,128)(2,1)} %grad_ref.1) | copy-start | bytes 688132

commit v2 on v1

v2 whole, which is shorter than its diff:
```python
import functools

import jax
import jax.numpy as jnp
from jax import lax
from jax.experimental import pallas as pl
from jax.experimental.pallas import tpu as pltpu
from jax.sharding import PartitionSpec as P

PACK = 8
BF = jnp.bfloat16
F32 = jnp.float32


def flip(index, bit):
    return index + bit - 2 * bit * ((index // bit) % 2)


def push(src, dst, send, recv, peer):
    copy = pltpu.make_async_remote_copy(
        src_ref=src,
        dst_ref=dst,
        send_sem=send,
        recv_sem=recv,
        device_id=peer,
        device_id_type=pl.DeviceIdType.MESH,
    )
    copy.start()
    return copy


def select(ids, first, lines, slot, cap):
    rows, tok = ids.shape
    local = ids - first
    owned = (local >= 0) & (local < lines * PACK) & (ids % PACK == slot)
    before = lax.broadcasted_iota(jnp.int32, (tok, tok), 0) < lax.broadcasted_iota(
        jnp.int32, (tok, tok), 1
    )
    rank = jnp.dot(
        jnp.where(owned, 1.0, 0.0).astype(BF),
        jnp.where(before, 1.0, 0.0).astype(BF),
        preferred_element_type=F32,
    )
    want = lax.broadcasted_iota(jnp.int32, (rows, tok), 0) % cap
    return owned & (rank.astype(jnp.int32) == want), local


def kernel(
    groups, segs, inside, chunk,
    ids_ref, table_ref, grad_ref,
    emb_ref, back_ref, hot_ref,
    ids_mine, ids_all, table, rows_out, rows_in, grads, back_out, part, halves, total,
    load_sem, ids_sem, raw_sem, grad_sem, fwd_sem, bwd_sem, seg_sem,
):
    dp = lax.axis_index("dp")
    seg = lax.axis_index("segment")
    lines, width = table.shape
    cap, tok = ids_mine.shape
    quarters = groups // PACK
    chunks = width // chunk
    half = tok // 2
    near = groups // 2
    base = (dp // near) * near
    mirror = (dp + near) % groups
    first = seg * lines * PACK
    core = seg % 2
    offsets = sorted(range(1, groups), key=lambda k: -min(k, groups - k))
    bits = [1 << b for b in range(segs.bit_length() - 1)]
    far = bits[::-1] if inside else []
    own = seg if inside else 0

    load_grad = pltpu.make_async_copy(grad_ref, grads.at[0, own], load_sem.at[0])
    load_grad.start()
    load = pltpu.make_async_copy(table_ref, table, load_sem.at[1])
    load.start()
    ids_mine[...] = jnp.broadcast_to(ids_ref[...], (cap, tok))
    barrier = pltpu.get_barrier_semaphore()
    for k in offsets:
        pl.semaphore_signal(
            barrier, inc=1, device_id={"dp": (dp + k) % groups},
            device_id_type=pl.DeviceIdType.MESH,
        )
    for b in bits:
        pl.semaphore_signal(
            barrier, inc=1, device_id={"segment": flip(seg, b)},
            device_id_type=pl.DeviceIdType.MESH,
        )
    load_grad.wait()
    pl.semaphore_wait(barrier, len(offsets) + len(bits))

    sent = []
    ids_copies = []
    for k in offsets:
        ids_copies.append(push(
            ids_mine, ids_all.at[dp], ids_sem.at[0, k], ids_sem.at[1, k],
            {"dp": (dp + k) % groups},
        ))
    raw = push(
        grads.at[0, own], grads.at[1, own], raw_sem.at[0], raw_sem.at[1], {"dp": mirror}
    )

    held = [[own], [own]]
    flying = [[], []]

    def gather_start(kind, level):
        for piece in held[kind]:
            n = len(sent_of[kind])
            copy = push(
                grads.at[kind, piece], grads.at[kind, piece],
                grad_sem.at[0, kind, n], grad_sem.at[1, kind, n],
                {"segment": flip(seg, far[level])},
            )
            sent_of[kind].append(copy)
            flying[kind].append(copy)

    def gather_wait(kind, level):
        for copy in flying[kind]:
            copy.wait_recv()
        flying[kind] = []
        held[kind] = held[kind] + [flip(piece, far[level]) for piece in held[kind]]

    sent_of = [[], []]
    if far:
        gather_start(0, 0)
    ids_all[dp] = ids_mine[...]

    slot_of = lax.broadcasted_iota(jnp.int32, (PACK * cap, tok), 0) // cap
    pick, _ = select(
        jnp.concatenate([ids_mine[...]] * PACK, axis=0), first, lines, slot_of, cap
    )
    scatter = jnp.where(pick, 1.0, 0.0).T.astype(BF)

    for copy in ids_copies:
        copy.wait_recv()
    named, local = select(
        ids_all[...].reshape(groups * cap, tok), first, lines, dp // quarters, cap
    )
    line = jnp.sum(
        jnp.where(named, (local // PACK + 1).astype(F32), 0.0), axis=1, keepdims=True
    ).astype(jnp.int32) - 1
    hot = jnp.where(
        lax.broadcasted_iota(jnp.int32, (groups * cap, lines), 1) == line, 1.0, 0.0
    ).astype(BF)
    hot_ref[...] = hot

    load.wait()
    fwd = []
    for f in range(chunks):
        cols = pl.ds(f * chunk, chunk)
        got = jnp.dot(hot_ref[...], table[:, cols], preferred_element_type=F32).astype(BF)
        rows_out[:, :, cols] = got.reshape(groups, cap, chunk)
        fwd.append([])
        for k in offsets:
            peer = (dp + k) % groups
            fwd[f].append(push(
                rows_out.at[peer, :, cols], rows_in.at[dp, :, cols],
                fwd_sem.at[0, k, f], fwd_sem.at[1, k, f], {"dp": peer},
            ))
    rows_in[dp] = rows_out[dp]

    slots_near = PACK // 2
    near_slot = base // quarters + lax.broadcasted_iota(
        jnp.int32, (slots_near * cap, tok), 0
    ) // cap
    depth = quarters * width
    piece_width = grads.shape[3]
    step = min(piece_width, width)
    bwd = []

    def dispatch(kind, group):
        pick, _ = select(
            jnp.concatenate([ids_all[group]] * slots_near, axis=0), first, lines, near_slot, cap
        )
        pick = jnp.where(pick, 1.0, 0.0).astype(BF)
        for at in range(0, depth, step):
            q, off = at // width, at % width
            inner = at % piece_width
            got = jnp.dot(
                pick, grads[kind, at // piece_width, :, inner:inner + step],
                preferred_element_type=F32,
            ).astype(BF)
            for r in range(slots_near):
                back_out[kind, r * quarters + q, :, off:off + step] = got[r * cap:(r + 1) * cap]
        for k in range(1, near):
            to = (dp - base + k) % near
            bwd.append(push(
                back_out.at[kind, to], back_ref.at[group],
                bwd_sem.at[0, kind, k], bwd_sem.at[1, kind, k], {"dp": base + to},
            ))
        back_ref[group] = back_out[kind, dp - base]

    for level in range(len(far)):
        if level > 0:
            gather_start(0, level)
        gather_wait(0, level)
    dispatch(0, dp)
    raw.wait_recv()
    for level in range(len(far)):
        gather_start(1, level)
        gather_wait(1, level)
    dispatch(1, mirror)

    tiles = [(f, q) for f in range(chunks) for q in range(quarters)]
    stages = len(bits) + 2
    moving = {}

    def seg_push(src, dst, level, n, bit):
        copy = push(
            src, dst, seg_sem.at[0, level, n], seg_sem.at[1, level, n],
            {"segment": flip(seg, bit)},
        )
        sent.append(copy)
        moving[n] = copy

    def advance(n, stage):
        f, q = tiles[n]
        at = q * width + f * chunk
        cols = pl.ds(at, chunk)
        if stage == 0:
            if q == 0:
                for copy in fwd[f]:
                    copy.wait_recv()
            got = jnp.concatenate(
                [rows_in[r * quarters + q, :, f * chunk:(f + 1) * chunk] for r in range(PACK)], axis=0
            )
            got = jnp.dot(scatter, got, preferred_element_type=F32).astype(BF)
            part[:, :, cols] = got.reshape(2, half, chunk)
            seg_push(part.at[1 - core, :, cols], halves.at[0, :, cols], 0, n, 1)
            return
        moving[n].wait_recv()
        if stage == stages - 1:
            return
        if stage == 1:
            total[0, :, cols] = part[core, :, cols] + halves[0, :, cols]
        else:
            total[stage - 1, :, cols] = total[stage - 2, :, cols] + halves[stage - 1, :, cols]
        src = total.at[stage - 1, :, cols]
        if stage < len(bits):
            seg_push(src, halves.at[stage, :, cols], stage, n, bits[stage])
        else:
            seg_push(src, emb_ref.at[core, :, cols], stage, n, 1)
            emb_ref[core, :, cols] = total[stage - 1, :, cols]

    for wave in range(len(tiles) + stages - 1):
        for stage in range(stages):
            if 0 <= wave - stage < len(tiles):
                advance(wave - stage, stage)

    for copy in bwd:
        copy.wait_recv()
    for copies in [sent, ids_copies, [raw], bwd] + sent_of + fwd:
        for copy in copies:
            copy.wait_send()


def body(token_ids, table, out_grad, groups, segs):
    lines, width = table.shape
    tok, piece = out_grad.shape
    depth = segs * piece
    cap = tok // PACK
    inside = piece % 128 == 0 and width % piece == 0
    if not inside:
        out_grad = lax.all_gather(out_grad, "segment", axis=1, tiled=True)
    pieces = segs if inside else 1
    chunk = width // 4 if width % 512 == 0 else width
    chunks = width // chunk
    levels = segs.bit_length() - 1
    vmem = pl.BlockSpec(memory_space=pltpu.VMEM)
    hbm = pl.BlockSpec(memory_space=pltpu.HBM)
    dma = pltpu.SemaphoreType.DMA
    emb, back, hot = pl.pallas_call(
        functools.partial(kernel, groups, segs, inside, chunk),
        out_shape=(
            jax.ShapeDtypeStruct((2, tok // 2, depth), BF),
            jax.ShapeDtypeStruct((groups, cap, width), BF),
            jax.ShapeDtypeStruct((groups * cap, lines), BF),
        ),
        in_specs=[vmem, hbm, hbm],
        out_specs=(vmem, vmem, vmem),
        scratch_shapes=[
            pltpu.VMEM((cap, tok), jnp.int32),
            pltpu.VMEM((groups, cap, tok), jnp.int32),
            pltpu.VMEM((lines, width), BF),
            pltpu.VMEM((groups, cap, width), BF),
            pltpu.VMEM((groups, cap, width), BF),
            pltpu.VMEM((2, pieces, tok, depth // pieces), BF),
            pltpu.VMEM((2, groups // 2, cap, width), BF),
            pltpu.VMEM((2, tok // 2, depth), BF),
            pltpu.VMEM((levels, tok // 2, depth), BF),
            pltpu.VMEM((levels, tok // 2, depth), BF),
            dma((2,)),
            dma((2, groups)),
            dma((2,)),
            dma((2, 2, segs)),
            dma((2, groups, chunks)),
            dma((2, 2, groups // 2)),
            dma((2, levels + 1, chunks * (groups // PACK))),
        ],
        compiler_params=pltpu.CompilerParams(
            collective_id=0, has_side_effects=True, vmem_limit_bytes=48 << 20
        ),
    )(token_ids[None, :], table, out_grad)
    grad = lax.dot_general(
        hot, back.reshape(groups * cap, width), (((0,), (0,)), ((), ())),
        preferred_element_type=F32,
    )
    return emb.reshape(tok, depth), grad.astype(BF)


def solution(mesh):
    placed = (P("dp"), P("segment", "dp"), P("dp", "segment"))
    return jax.shard_map(
        functools.partial(body, groups=mesh.shape["dp"], segs=mesh.shape["segment"]),
        mesh=mesh,
        in_specs=placed,
        out_specs=(P("dp", None), P("segment", "dp")),
        check_vma=False,
    )
```

time: 65 us -> 59.3 us (0.912)
  Pallas kernels: 55.8 us -> 50.2 us
    pallas_call x1, Pallas kernels: 55.8 us -> 50.2 us  [body(): pl.pallas_call(functools.partial(kernel, groups, segs, inside, chunk), ou...]
    broadcast_in_dim x1 -> x0, local copies, waits for them, and re-layouts: 0.66 us -> none  [body(): jnp.broadcast_to(token_ids[None, :], (cap, tok))]
    unnamed x3 -> x5, local copies, waits for them, and re-layouts: 1.86 us -> 2.51 us
where the time goes in v2:
time: 59.3 us; the launch traced here: 59.2 us
  Pallas kernels  50.2 us (85%)
  matrix products  5.85 us (10%)
  local copies, waits for them, and re-layouts  2.51 us (4%)
  between operations  0.65 us (1%)
    pallas_call x1, Pallas kernels, body(): pl.pallas_call(functools.partial(kernel, groups, segs, inside, chunk), ou...  50.2 us
    dot_general x1, matrix products, body(): lax.dot_general(hot, back.reshape(groups * cap, width), (((0,), (0,)), ((...  5.85 us
    unnamed x5, local copies, waits for them, and re-layouts  2.51 us

profile of v2, /device:TPU:0, one launch (start us, length us, event | category | flops | bytes accessed | tf_op | source)
XLA Modules:
  0.0 59.2 jit_solution(13461936982661401486)
XLA Ops:
  0.6 0.0 copy-start
  0.6 0.9 %copy-done = bf16[128,896]{1,0:T(8,128)(2,1)S(1)} copy-done((bf16[128,896]{1,0:T(8,128)(2,1)S(1)}, bf16[128,896]{1,0:T(8,128)(2,1)}, u32[]{:S(2)}) %copy-start) | copy-done | bytes 229400
  1.6 0.0 copy-start.1
  1.6 0.7 %copy-done.1 = s32[128]{0:T(128)S(1)} copy-done((s32[128]{0:T(128)S(1)}, s32[128]{0:T(128)}, u32[]{:S(2)}) %copy-start.1) | copy-done | bytes 536
  2.2 50.2 %shard_map.50 = (bf16[2,64,3584]{2,1,0:T(8,128)(2,1)S(1)}, bf16[8,16,3584]{2,1,0:T(8,128)(2,1)S(1)}, bf16[128,1188]{1,0:T(8,128)(2,1)S(1)}) custom-call(s32[1,128]{1,0:T(1,128)S(1)} %bitcast.7, bf16[1188,3584]{1,0:T(8,128)(2,1)} %table_ref.1, bf16[128,896]{1,0:T(8,128)(2,1)S(1)} %copy-done), custom_call_target="tpu_custom_call" | custom-call | tf_op jit(solution)/shard_map/pallas_call | solution.py:271
  52.4 5.9 %convolution_convert_fusion = bf16[1188,3584]{1,0:T(8,128)(2,1)} fusion(bf16[128,1188]{1,0:T(8,128)(2,1)S(1)} %get-tuple-element.6, bf16[128,3584]{1,0:T(8,128)(2,1)S(1)} %bitcast.5), kind=kOutput, calls=%fused_computation | convolution fusion | flops 1094252544 | bytes 9737216 | tf_op jit(solution)/shard_map/dot_general | solution.py:303
  58.3 0.9 %copy.6 = bf16[128,3584]{1,0:T(8,128)(2,1)} copy(bf16[128,3584]{1,0:T(8,128)(2,1)S(1)} %bitcast.6) | data formatting | bytes 1835008
Async XLA Ops:
  0.6 0.9 %copy-start = (bf16[128,896]{1,0:T(8,128)(2,1)S(1)}, bf16[128,896]{1,0:T(8,128)(2,1)}, u32[]{:S(2)}) copy-start(bf16[128,896]{1,0:T(8,128)(2,1)} %grad_ref.1) | copy-start | bytes 688132
  1.6 0.7 %copy-start.1 = (s32[128]{0:T(128)S(1)}, s32[128]{0:T(128)}, u32[]{:S(2)}) copy-start(s32[128]{0:T(128)} %param.3) | copy-start | bytes 1540

commit v3 on v2

--- a/solution.py
+++ b/solution.py
@@ -95,6 +95,7 @@
             ids_mine, ids_all.at[dp], ids_sem.at[0, k], ids_sem.at[1, k],
             {"dp": (dp + k) % groups},
         ))
+
     raw = push(
         grads.at[0, own], grads.at[1, own], raw_sem.at[0], raw_sem.at[1], {"dp": mirror}
     )
@@ -120,8 +121,6 @@
         held[kind] = held[kind] + [flip(piece, far[level]) for piece in held[kind]]
 
     sent_of = [[], []]
-    if far:
-        gather_start(0, 0)
     ids_all[dp] = ids_mine[...]
 
     slot_of = lax.broadcasted_iota(jnp.int32, (PACK * cap, tok), 0) // cap
@@ -132,6 +131,8 @@
 
     for copy in ids_copies:
         copy.wait_recv()
+    if far:
+        gather_start(0, 0)
     named, local = select(
         ids_all[...].reshape(groups * cap, tok), first, lines, dp // quarters, cap
     )
@@ -143,6 +144,13 @@
     ).astype(BF)
     hot_ref[...] = hot
 
+    def fetch(f, n, peer):
+        cols = pl.ds(f * chunk, chunk)
+        fwd[f].append(push(
+            rows_out.at[peer, :, cols], rows_in.at[dp, :, cols],
+            fwd_sem.at[0, n, f], fwd_sem.at[1, n, f], {"dp": peer},
+        ))
+
     load.wait()
     fwd = []
     for f in range(chunks):
@@ -150,12 +158,11 @@
         got = jnp.dot(hot_ref[...], table[:, cols], preferred_element_type=F32).astype(BF)
         rows_out[:, :, cols] = got.reshape(groups, cap, chunk)
         fwd.append([])
-        for k in offsets:
-            peer = (dp + k) % groups
-            fwd[f].append(push(
-                rows_out.at[peer, :, cols], rows_in.at[dp, :, cols],
-                fwd_sem.at[0, k, f], fwd_sem.at[1, k, f], {"dp": peer},
-            ))
+        for k in range(1, near):
+            fetch(f, k, base + (dp - base + k) % near)
+    for f in range(chunks):
+        for k in range(near):
+            fetch(f, near + k, (near - base) + (dp - base + k) % near)
     rows_in[dp] = rows_out[dp]
 
     slots_near = PACK // 2
@@ -194,12 +201,6 @@
             gather_start(0, level)
         gather_wait(0, level)
     dispatch(0, dp)
-    raw.wait_recv()
-    for level in range(len(far)):
-        gather_start(1, level)
-        gather_wait(1, level)
-    dispatch(1, mirror)
-
     tiles = [(f, q) for f in range(chunks) for q in range(quarters)]
     stages = len(bits) + 2
     moving = {}
@@ -242,6 +243,15 @@
             emb_ref[core, :, cols] = total[stage - 1, :, cols]
 
     for wave in range(len(tiles) + stages - 1):
+        if wave == 0:
+            raw.wait_recv()
+            if far:
+                gather_start(1, 0)
+            for level in range(len(far)):
+                gather_wait(1, level)
+                if level + 1 < len(far):
+                    gather_start(1, level + 1)
+            dispatch(1, mirror)
         for stage in range(stages):
             if 0 <= wave - stage < len(tiles):
                 advance(wave - stage, stage)

time: 59.3 us -> 57.2 us (0.965)
  Pallas kernels: 50.2 us -> 48.1 us
    pallas_call x1, Pallas kernels: 50.2 us -> 48.1 us  [body(): pl.pallas_call(functools.partial(kernel, groups, segs, inside, chunk), ou...]
where the time goes in v3:
time: 57.2 us; the launch traced here: 57.1 us
  Pallas kernels  48.1 us (84%)
  matrix products  5.85 us (10%)
  local copies, waits for them, and re-layouts  2.51 us (4%)
  between operations  0.65 us (1%)
    pallas_call x1, Pallas kernels, body(): pl.pallas_call(functools.partial(kernel, groups, segs, inside, chunk), ou...  48.1 us
    dot_general x1, matrix products, body(): lax.dot_general(hot, back.reshape(groups * cap, width), (((0,), (0,)), ((...  5.85 us
    unnamed x5, local copies, waits for them, and re-layouts  2.51 us

profile of v3, /device:TPU:0, one launch (start us, length us, event | category | flops | bytes accessed | tf_op | source)
XLA Modules:
  0.0 57.1 jit_solution(18321742898524752093)
XLA Ops:
  0.6 0.0 copy-start
  0.6 0.9 %copy-done = bf16[128,896]{1,0:T(8,128)(2,1)S(1)} copy-done((bf16[128,896]{1,0:T(8,128)(2,1)S(1)}, bf16[128,896]{1,0:T(8,128)(2,1)}, u32[]{:S(2)}) %copy-start) | copy-done | bytes 229400
  1.6 0.0 copy-start.1
  1.6 0.7 %copy-done.1 = s32[128]{0:T(128)S(1)} copy-done((s32[128]{0:T(128)S(1)}, s32[128]{0:T(128)}, u32[]{:S(2)}) %copy-start.1) | copy-done | bytes 536
  2.2 48.1 %shard_map.50 = (bf16[2,64,3584]{2,1,0:T(8,128)(2,1)S(1)}, bf16[8,16,3584]{2,1,0:T(8,128)(2,1)S(1)}, bf16[128,1188]{1,0:T(8,128)(2,1)S(1)}) custom-call(s32[1,128]{1,0:T(1,128)S(1)} %bitcast.7, bf16[1188,3584]{1,0:T(8,128)(2,1)} %table_ref.1, bf16[128,896]{1,0:T(8,128)(2,1)S(1)} %copy-done), custom_call_target="tpu_custom_call" | custom-call | tf_op jit(solution)/shard_map/pallas_call | solution.py:281
  50.3 5.9 %convolution_convert_fusion = bf16[1188,3584]{1,0:T(8,128)(2,1)} fusion(bf16[128,1188]{1,0:T(8,128)(2,1)S(1)} %get-tuple-element.6, bf16[128,3584]{1,0:T(8,128)(2,1)S(1)} %bitcast.5), kind=kOutput, calls=%fused_computation | convolution fusion | flops 1094252544 | bytes 9737216 | tf_op jit(solution)/shard_map/dot_general | solution.py:313
  56.2 0.9 %copy.6 = bf16[128,3584]{1,0:T(8,128)(2,1)} copy(bf16[128,3584]{1,0:T(8,128)(2,1)S(1)} %bitcast.6) | data formatting | bytes 1835008
Async XLA Ops:
  0.6 0.9 %copy-start = (bf16[128,896]{1,0:T(8,128)(2,1)S(1)}, bf16[128,896]{1,0:T(8,128)(2,1)}, u32[]{:S(2)}) copy-start(bf16[128,896]{1,0:T(8,128)(2,1)} %grad_ref.1) | copy-start | bytes 688132
  1.6 0.7 %copy-start.1 = (s32[128]{0:T(128)S(1)}, s32[128]{0:T(128)}, u32[]{:S(2)}) copy-start(s32[128]{0:T(128)} %param.3) | copy-start | bytes 1540
